TPU v7x, 256 devices: a 4x2x16 block of a 4x16x16 slice. The times are simulated.
256 devices in a mesh: groups: 2 (over y), seq: 16 (over z), head: 8 (over x, core).
Axes of the slice: x: 4, y: 2, z: 16, core: 2. Of those that a mesh axis runs over, the one named last changes fastest.
The devices are a block of a 4x16x16 slice.
Arguments:
- residual: bfloat16 [16384, 2560], P(('groups', 'seq'), 'head'), parts along dimension 0, may hold values from -6 to 6
- x_in: bfloat16 [16384, 5120], P(('groups', 'seq'), 'head'), parts along dimension 0, may hold values from -6 to 6
- bc_in: bfloat16 [16384, 256], P(('groups', 'seq')), parts along dimension 0, may hold values from -1.5 to 1.5
- z_in: bfloat16 [16384, 5120], P(('groups', 'seq'), 'head'), parts along dimension 0, may hold values from -6 to 6
- dt_raw: float32 [80, 16384], P('head', ('groups', 'seq')), parts along dimension 1, may hold values from -5 to 5
- dt_bias: float32 [80], P('head'), may hold values from -3 to 0
- decay_rate: float32 [80], P('head'), may hold values from 0.0003 to 0.15
- d_skip: float32 [80], P('head'), may hold values from 1 to 4
- conv_x_weight: bfloat16 [4, 5120], P(None, 'head'), may hold values from -3 to 3
- conv_x_bias: bfloat16 [5120], P('head'), may hold values from -3 to 3
- conv_bc_weight: bfloat16 [4, 256], replicated, may hold values from -3 to 3
- conv_bc_bias: bfloat16 [256], replicated, may hold values from -3 to 3
- norm_gain: bfloat16 [5120], P('head'), may hold values from 0.5 to 1.5
- out_weight: bfloat16 [5120, 2560], P('head'), may hold values from -0.078125 to 0.078125
- final_gain: bfloat16 [2560], replicated, may hold values from 0.5 to 1.5
- lm_weight: bfloat16 [2560, 25600], P('seq', 'head'), may hold values from -15.811388 to 15.811388
- targets: int32 [16384], P(('groups', 'seq')), parts along dimension 0, may hold values from 0 to 25599
- doc_lengths: int32 [32], P('groups'), parts along dimension 0, may hold values from 1 to 1536, as said below
Outputs:
- block_out: bfloat16 [16384, 2560], P(('groups', 'seq'), 'head'), parts along dimension 0
- doc_loss: float32 [32], P('groups'), parts along dimension 0
There are 2 independent parts, one for each index of `groups`. A program takes and returns all parts, laid end to end along the dimension named above; an argument that names none is the same for every part. Nothing has to cross between parts.
Inputs may be any that keep to these rules, and one draw needn't show every extreme that they name: `doc_lengths`: the lengths of a group's 16 documents, in the order in which they are packed into its 8192 tokens; they sum to 8192.
All inputs are finite; a program needn't handle non-finite values.
Results may differ from a plain program's by a relative error of at most 0.00145.
The roundings to bfloat16 on the way count: a program that leaves them out, or rounds other values in their place, can miss the bound.
Values may be sent and summed in bfloat16 or wider, within the bound.
No kernel may reach another device: no remote copies, remote signals or barrier semaphores. Data moves between devices by JAX's collectives and lax.ppermute only.
A program may use at most 128 MiB of HBM per device.

v0:
```python
import jax
import jax.numpy as jnp
from jax import lax
from jax.sharding import PartitionSpec as P

D = 2560
HEAD_SIZE = 64
STATE = 128
KERNEL = 4
SPAN = 256
INNER = 5120
EPSILON = 1e-05
HIGH = lax.Precision.HIGHEST


def shifted(array, axis, by):
    length = lax.axis_size(axis)
    pairs = [(i, i + by) for i in range(length) if 0 <= i + by < length]
    return lax.ppermute(array, axis, pairs)


def entering(part, axis, combine, identity):
    place = lax.axis_index(axis)
    gathered = jax.tree.map(lambda a: lax.all_gather(a, axis), part)
    state = jax.tree.map(lambda a, e: jnp.zeros_like(a) + jnp.asarray(e, a.dtype), part, identity)

    def one(lap, state):
        return combine(
            state, jax.tree.map(lambda a: lax.dynamic_index_in_dim(a, lap, 0, False), gathered)
        )

    return lax.fori_loop(0, place, one, state)


def cut_along(array, dim, length):
    shape = array.shape
    blocks = array.reshape(*shape[:dim], length, shape[dim] // length, *shape[dim + 1 :])
    return jnp.moveaxis(blocks, dim, 0)


def sent_and_summed(array, axis, dim):
    blocks = cut_along(array, dim, lax.axis_size(axis))
    arrived = lax.all_to_all(blocks, axis, split_axis=0, concat_axis=0, tiled=True)
    return arrived.sum(axis=0)


def joined_along(blocks, dim):
    shape = list(blocks.shape[1:])
    shape[dim] *= blocks.shape[0]
    return jnp.moveaxis(blocks, 0, dim).reshape(shape)


def from_everyone(array, axis):
    length = lax.axis_size(axis)
    return lax.all_to_all(
        jnp.broadcast_to(array[None], (length, *array.shape)), axis, 0, 0, tiled=True
    )


def gather_directly(array, axis, dim):
    return joined_along(from_everyone(array, axis), dim)


def gathered_once(array, axis):
    leaves = jax.tree.leaves(array)
    sequence = sorted(range(len(leaves)), key=lambda k: -leaves[k].size)
    width = (1, *leaves[sequence[0]].shape)[-1]
    lines = [
        jnp.pad(leaves[k].reshape(-1), (0, -leaves[k].size % width)).reshape(-1, width)
        for k in sequence
    ]
    both, at, found = (lax.all_gather(jnp.concatenate(lines), axis), 0, {})
    for k, line in zip(sequence, lines):
        section = both[:, at : at + len(line)].reshape(len(both), -1)
        found[k] = section[:, : leaves[k].size].reshape(-1, *leaves[k].shape)
        at += len(line)
    numbers = iter(range(len(leaves)))
    return jax.tree.map(lambda _: found[next(numbers)], array)


def joined_2(part, axis, combine):
    gathered = gathered_once(part, axis)

    def take(source):
        return jax.tree.map(lambda a: lax.dynamic_index_in_dim(a, source, 0, False), gathered)

    return lax.fori_loop(
        1, lax.axis_size(axis), lambda source, state: combine(state, take(source)), take(0)
    )


def over_copies(array, axis):
    return from_everyone(array, axis).sum(axis=0)


def document_of(positions, doc_lengths):
    starts = jnp.cumsum(doc_lengths) - doc_lengths
    return jnp.sum((positions[:, None] >= starts[None, :]).astype(jnp.int32), axis=1) - 1


def causal_conv(signal, rim_rows, weight, bias, positions, doc_ids, doc_lengths):
    length = signal.shape[0]
    taps = weight.shape[0]
    joined = jnp.concatenate([rim_rows, signal], axis=0).astype(jnp.float32)
    total = jnp.zeros(signal.shape, jnp.float32) + bias.astype(jnp.float32)[None, :]
    for offset in range(taps):
        lag = taps - 1 - offset
        source = document_of(positions - lag, doc_lengths)
        same = (source == doc_ids).astype(jnp.float32)
        total = (
            total
            + weight[offset].astype(jnp.float32)[None, :]
            * joined[offset : offset + length]
            * same[:, None]
        )
    return jax.nn.silu(total).astype(jnp.bfloat16)


def span_step(state, pieces, rates):
    signal, bmat, cmat, steps, doc_ids, doc_prev = pieces
    signal = signal.astype(jnp.float32)
    bmat = bmat.astype(jnp.float32)
    cmat = cmat.astype(jnp.float32)
    climb = jnp.cumsum(steps * rates[:, None], axis=1)
    extent = doc_ids.shape[0]
    order = jnp.arange(extent, dtype=jnp.int32)
    inside = (doc_ids[:, None] == doc_ids[None, :]) & (order[:, None] >= order[None, :])
    gap = climb[:, :, None] - climb[:, None, :]
    decay = jnp.where(inside[None], jnp.exp(-jnp.where(inside[None], gap, 0.0)), 0.0)
    scores = jnp.dot(cmat, bmat.T, precision=HIGH)
    weights = decay * scores[None] * steps[:, None, :]
    output = jnp.einsum("hts,shp->thp", weights, signal, precision=HIGH)
    carried = (doc_ids == doc_prev).astype(jnp.float32)
    entry = jnp.exp(-climb) * carried[None, :]
    output = output + jnp.einsum("tn,hpn->thp", cmat, state, precision=HIGH) * entry.T[:, :, None]
    last = doc_ids[extent - 1]
    tail = (
        jnp.exp(climb - climb[:, extent - 1 :])
        * (doc_ids == last).astype(jnp.float32)[None, :]
        * steps
    )
    kept = jnp.exp(-climb[:, extent - 1]) * (last == doc_prev).astype(jnp.float32)
    fresh = jnp.einsum("hs,shp,sn->hpn", tail, signal, bmat, precision=HIGH)
    return (kept[:, None, None] * state + fresh, output)


def chain_combine(earlier, later):
    return (earlier[0] * later[0], later[0][:, None, None] * earlier[1] + later[1])


def softmax_combine(first_part, second_part):
    peak = jnp.maximum(first_part[0], second_part[0])
    total = first_part[1] * jnp.exp(first_part[0] - peak) + second_part[1] * jnp.exp(
        second_part[0] - peak
    )
    return (peak, total, first_part[2] + second_part[2])


def local(
    residual,
    x_in,
    bc_in,
    z_in,
    dt_raw,
    dt_bias,
    decay_rate,
    d_skip,
    conv_x_weight,
    conv_x_bias,
    conv_bc_weight,
    conv_bc_bias,
    norm_gain,
    out_weight,
    final_gain,
    lm_weight,
    targets,
    doc_lengths,
):
    length = x_in.shape[0]
    inner_here = x_in.shape[1]
    heads_here = dt_raw.shape[0]
    seq_rank = lax.axis_index("seq")
    head_rank = lax.axis_index("head")
    offset_here = seq_rank * length
    positions = offset_here + jnp.arange(length, dtype=jnp.int32)
    doc_ids = document_of(positions, doc_lengths)
    margin = KERNEL - 1
    x_rim, bc_rim = shifted((x_in[length - margin :], bc_in[length - margin :]), "seq", 1)
    signal = causal_conv(x_in, x_rim, conv_x_weight, conv_x_bias, positions, doc_ids, doc_lengths)
    keys_queries = causal_conv(
        bc_in, bc_rim, conv_bc_weight, conv_bc_bias, positions, doc_ids, doc_lengths
    )
    steps = jax.nn.softplus(dt_raw + dt_bias[:, None])
    blocks = length // SPAN
    block_starts = offset_here + jnp.arange(blocks, dtype=jnp.int32) * SPAN
    pieces = (
        signal.reshape(blocks, SPAN, heads_here, HEAD_SIZE),
        keys_queries[:, :STATE].reshape(blocks, SPAN, STATE),
        keys_queries[:, STATE:].reshape(blocks, SPAN, STATE),
        steps.reshape(heads_here, blocks, SPAN).transpose(1, 0, 2),
        doc_ids.reshape(blocks, SPAN),
        document_of(block_starts - 1, doc_lengths),
    )

    def advance(state, piece):
        return span_step(state, piece, decay_rate)

    local_end, outputs = lax.scan(
        advance, jnp.zeros((heads_here, HEAD_SIZE, STATE), jnp.float32), pieces
    )
    outputs = outputs.reshape(length, heads_here, HEAD_SIZE)
    before = document_of(jnp.reshape(offset_here - 1, (1,)), doc_lengths)[0]
    carried = (doc_ids == before).astype(jnp.float32)
    climb = jnp.cumsum(steps * decay_rate[:, None], axis=1)
    through = jnp.exp(-climb[:, length - 1]) * carried[length - 1]
    identity = (jnp.ones_like(through), jnp.zeros_like(local_end))
    incoming = entering((through, local_end), "seq", chain_combine, identity)[1]
    entry = jnp.exp(-climb) * carried[None, :]
    cmat = keys_queries[:, STATE:].astype(jnp.float32)
    outputs = (
        outputs + jnp.einsum("tn,hpn->thp", cmat, incoming, precision=HIGH) * entry.T[:, :, None]
    )
    mixed = outputs + d_skip[None, :, None] * signal.reshape(length, heads_here, HEAD_SIZE).astype(
        jnp.float32
    )
    gated = mixed.reshape(length, inner_here) * jax.nn.silu(z_in.astype(jnp.float32))
    square_sum = lax.psum(jnp.sum(gated * gated, axis=1), "head")
    scale = lax.rsqrt(square_sum / INNER + EPSILON)
    normed = (gated * scale[:, None] * norm_gain.astype(jnp.float32)[None, :]).astype(jnp.bfloat16)
    partial_value = jnp.dot(normed, out_weight, preferred_element_type=jnp.float32)
    share = residual.shape[1]
    projected = sent_and_summed(partial_value, "head", 1)
    block_out = (residual.astype(jnp.float32) + projected).astype(jnp.bfloat16)
    widened = block_out.astype(jnp.float32)
    square_total = lax.psum(jnp.sum(widened * widened, axis=1), "head")
    gain_part = lax.dynamic_slice_in_dim(final_gain, head_rank * share, share, 0)
    final_scale = lax.rsqrt(square_total / D + EPSILON)
    hidden_part = (widened * final_scale[:, None] * gain_part.astype(jnp.float32)[None, :]).astype(
        jnp.bfloat16
    )
    hidden = gather_directly(hidden_part, "head", 1)
    vocab_here = lm_weight.shape[1]
    logits = jnp.dot(
        hidden,
        lax.all_gather(lm_weight, "seq", axis=0, tiled=True),
        preferred_element_type=jnp.float32,
    )
    peak = jnp.max(logits, axis=1)
    total = jnp.sum(jnp.exp(logits - peak[:, None]), axis=1)
    local_target = targets - head_rank * vocab_here
    column = jnp.arange(vocab_here, dtype=jnp.int32)
    picked = jnp.sum(jnp.where(column[None, :] == local_target[:, None], logits, 0.0), axis=1)
    peak_all, total_all, picked_all = joined_2((peak, total, picked), "head", softmax_combine)
    losses = peak_all + jnp.log(total_all) - picked_all
    member = (
        doc_ids[:, None] == jnp.arange(doc_lengths.shape[0], dtype=jnp.int32)[None, :]
    ).astype(jnp.float32)
    sums = over_copies(jnp.dot(losses, member, precision=HIGH), "seq")
    return (block_out, sums / doc_lengths.astype(jnp.float32))


def solution(mesh):
    in_specs = (
        P(("groups", "seq"), "head"),
        P(("groups", "seq"), "head"),
        P(("groups", "seq"), None),
        P(("groups", "seq"), "head"),
        P("head", ("groups", "seq")),
        P("head"),
        P("head"),
        P("head"),
        P(None, "head"),
        P("head"),
        P(),
        P(),
        P("head"),
        P("head", None),
        P(),
        P("seq", "head"),
        P(("groups", "seq")),
        P("groups"),
    )
    out_specs = (P(("groups", "seq"), "head"), P("groups"))
    return jax.shard_map(local, mesh=mesh, in_specs=in_specs, out_specs=out_specs, check_vma=False)
```

profile of v0, /device:TPU:33, one launch (start us, length us, event | category | flops | bytes accessed | tf_op | source)
XLA Modules:
  0.0 454.0 jit_solution(4214907796771070101)
XLA Ops:
  8.7 5.8 %collective-permute-start = (bf16[3,640]{1,0:T(4,128)(2,1)}, bf16[3,640]{1,0:T(4,128)(2,1)}, u32[]{:S(2)}, u32[]{:S(2)}) collective-permute-start(bf16[3,640]{1,0:T(4,128)(2,1)} %slice.103), channel_id=1, source_target_pairs={{0,8},{8,16},{16,24},{24,32},{32,40},{40,48},{48,56},{56,64},{64,7... | collective-permute-start | bytes 11528 | tf_op jit(solution)/shard_map/ppermute | solution.py:19
  15.2 3.8 collective-permute-start.1
  41.5 80.0 %while.46 = (s32[]{:T(128)}, f32[10,64,128]{2,1,0:T(8,128)}, f32[2,256,10,64]{1,0,3,2:T(2,128)}, f32[2,10,256]{2,0,1:T(2,128)}, f32[10]{0:T(128)}, /*index=5*/s3...) while((s32[]{:T(128)}, f32[10,64,128]{2,1,0:T(8,128)}, ...), condition=%wide.region_9.10_spmd.clone, body=%wide.region_6.9_spmd.clone.sunk | while | flops 1028866112 | bytes 7581990 | solution.py:208
  51.7 4.0 fusion.117
  63.0 14.2 %dynamic_update_slice.6 = f32[2,256,10,64]{1,0,3,2:T(2,128)} dynamic-update-slice(f32[2,256,10,64]{1,0,3,2:T(2,128)} %get-tuple-element.624, f32[1,256,10,64]{1,0,3,2:T(1,128)} %copy.129, s32[]{:T(128)} %get-tuple-element.622, s32[]{:T(128)} %constant.152.clone.1..sunk.2, s32[]{:T(128)} %constant.152.clone.1..sunk.2, s32[]{:T(128)} %constant.152.clone.1..sunk.2) | dynamic-update-slice | bytes 1310724 | tf_op jit(solution)/shard_map/while/body/jit(dynamic_update_index_in_dim)/dynamic_update_slice | solution.py:208
  91.6 4.0 fusion.117
  103.0 14.2 %dynamic_update_slice.6 = f32[2,256,10,64]{1,0,3,2:T(2,128)} dynamic-update-slice(f32[2,256,10,64]{1,0,3,2:T(2,128)} %get-tuple-element.624, f32[1,256,10,64]{1,0,3,2:T(1,128)} %copy.129, s32[]{:T(128)} %get-tuple-element.622, s32[]{:T(128)} %constant.152.clone.1..sunk.2, s32[]{:T(128)} %constant.152.clone.1..sunk.2, s32[]{:T(128)} %constant.152.clone.1..sunk.2) | dynamic-update-slice | bytes 1310724 | tf_op jit(solution)/shard_map/while/body/jit(dynamic_update_index_in_dim)/dynamic_update_slice | solution.py:208
  126.8 39.9 %all-reduce = f32[160]{0:T(256)S(1)} all-reduce(f32[160]{0:T(256)S(1)} %dynamic-update-slice), channel_id=2, replica_groups=mesh['groups'=2,'seq'=16,'head'=8] {'seq'}, use_global_device_ids=true, to_apply=%add | all-reduce | flops 160 | bytes 1280
  169.8 3.2 reshape.296
  173.0 32.3 %all-gather.9.cloned.1.call-done = f32[160,64,128]{2,1,0:T(8,128)} async-done(((f32[10,64,128]{2,1,0:T(8,128)}), f32[160,64,128]{2,1,0:T(8,128)}) %all-gather.9.cloned.1.call-update) | async-done | bytes 5242896 | tf_op jit(solution)/shard_map/all_gather | solution.py:24
  207.0 3.7 fusion.46
  210.8 2.8 copy.90
  215.5 20.6 %psum.14 = f32[512]{0:T(512)S(1)} all-reduce(f32[512]{0:T(512)S(1)} %multiply_reduce_fusion), channel_id=1, replica_groups=mesh['groups'=2,'seq'=16,'head'=8] {'head'}, use_global_device_ids=true, to_apply=%region_16.17 | all-reduce | flops 512 | bytes 4096 | tf_op jit(solution)/shard_map/psum | solution.py:227
  236.2 6.4 %fusion.61 = f32[512,2560]{0,1:T(8,128)} fusion(bf16[640,2560]{1,0:T(8,128)(2,1)S(1)} %copy-done, f32[640]{0:T(1024)S(1)} %convert_element_type.158, f32[512]{0:T(512)S(1)} %add_rsqrt_fusion.1, f32[512,640]{1,0:T(8,128)} %copy.90, bf16[512,640]{1,0:T(8,128)(2,1)} %param.27), kind=kOutput, calls=%fused_computation.97 | convolution fusion | flops 1680670720 | bytes 10490368 | tf_op jit(solution)/shard_map/dot_general | solution.py:230
  242.5 5.2 %all-to-all-start = ((f32[8,512,320]{1,2,0:T(8,128)}), f32[8,512,320]{1,2,0:T(8,128)}, u32[]{:S(2)}, u32[]{:S(2)}) async-start(f32[8,512,320]{1,2,0:T(8,128)} %bitcast.151), calls=%async_computation | async-start | bytes 10485760 | tf_op jit(solution)/shard_map/all_to_all | solution.py:43
  248.5 59.3 %all-to-all-done = f32[8,512,320]{1,2,0:T(8,128)} async-done(((f32[8,512,320]{1,2,0:T(8,128)}), f32[8,512,320]{1,2,0:T(8,128)}, u32[]{:S(2)}, u32[]{:S(2)}) %all-to-all-start) | async-done | bytes 5242912 | tf_op jit(solution)/shard_map/all_to_all | solution.py:43
  307.9 4.0 reduce_sum.118
  313.9 13.2 %psum.15 = f32[512]{0:T(512)S(1)} all-reduce(f32[512]{0:T(512)S(1)} %get-tuple-element.424), channel_id=1, replica_groups=mesh['groups'=2,'seq'=16,'head'=8] {'head'}, use_global_device_ids=true, to_apply=%region_19.20 | all-reduce | flops 512 | bytes 4096 | tf_op jit(solution)/shard_map/psum | solution.py:235
  329.9 5.8 %all-to-all-start.1 = ((bf16[8,512,320]{1,2,0:T(8,128)(2,1)}), bf16[8,512,320]{1,2,0:T(8,128)(2,1)}, u32[]{:S(2)}, u32[]{:S(2)}) async-start(bf16[8,512,320]{1,2,0:T(8,128)(2,1)} %broadcast_in_dim.26), calls=%async_computation.1 | async-start | bytes 5242880 | tf_op jit(solution)/shard_map/all_to_all | solution.py:55
  335.7 32.0 %all-to-all-done.1 = bf16[8,512,320]{1,2,0:T(8,128)(2,1)} async-done(((bf16[8,512,320]{1,2,0:T(8,128)(2,1)}), bf16[8,512,320]{1,2,0:T(8,128)(2,1)}, u32[]{:S(2)}, u32[]{:S(2)}) %all-to-all-start.1) | async-done | bytes 2621472 | tf_op jit(solution)/shard_map/all_to_all | solution.py:55
  367.7 27.6 %all-gather.7.cloned.1.call-done = bf16[2560,3200]{1,0:T(8,128)(2,1)} async-done(((bf16[160,3200]{1,0:T(8,128)(2,1)}), bf16[2560,3200]{1,0:T(8,128)(2,1)}) %all-gather.7.cloned.1.call-update) | async-done | bytes 16384016 | tf_op jit(solution)/shard_map/all_gather | solution.py:245
  395.3 14.5 %fusion.89 = (f32[512]{0:T(512)S(1)}, f32[512,3200]{1,0:T(8,128)S(1)}) fusion(bf16[512,2560]{0,1:T(8,128)(2,1)} %bitcast.23, bf16[2560,3200]{1,0:T(8,128)(2,1)} %all-gather.7.cloned.1.call-done), kind=kOutput, calls=%fused_computation.170 | convolution fusion | flops 8390245888 | bytes 25561088 | tf_op jit(solution)/shard_map/dot_general | solution.py:243
  411.8 13.9 %all-gather.3 = f32[8,3,512]{2,1,0:T(4,128)S(1)} all-gather(f32[1,3,512]{2,1,0:T(4,128)S(1)} %maximum_bitcast_fusion), channel_id=4, replica_groups=mesh['groups'=2,'seq'=16,'head'=8] {'head'}, dimensions={0}, use_global_device_ids=true | all-gather | bytes 55296 | tf_op jit(solution)/shard_map/all_gather | solution.py:72
  426.8 19.8 %all_to_all.16 = f32[16,1,16]{2,1,0:T(1,128)S(1)} all-to-all(f32[16,1,16]{2,1,0:T(1,128)S(1)} %broadcast_in_dim.28), channel_id=1, replica_groups=mesh['groups'=2,'seq'=16,'head'=8] {'seq'}, dimensions={0} | all-to-all | bytes 2048 | tf_op jit(solution)/shard_map/all_to_all | solution.py:55
  (201 shorter events, 85.2 us)
Async XLA Ops:
  7.2 229.0 %copy-start = (bf16[640,2560]{1,0:T(8,128)(2,1)S(1)}, bf16[640,2560]{1,0:T(8,128)(2,1)}, u32[]{:S(2)}) copy-start(bf16[640,2560]{1,0:T(8,128)(2,1)} %param.37) | copy-start | bytes 9830404
  7.2 198.1 %all-gather.9.cloned.1.call-start = ((), (), s32[]{:S(2)}) async-start(), calls=%async_computation.4 | async-start | bytes 5570560 | tf_op jit(solution)/shard_map/all_gather | solution.py:24
  8.7 23.1 %collective-permute-start = (bf16[3,640]{1,0:T(4,128)(2,1)}, bf16[3,640]{1,0:T(4,128)(2,1)}, u32[]{:S(2)}, u32[]{:S(2)}) collective-permute-start(bf16[3,640]{1,0:T(4,128)(2,1)} %slice.103), channel_id=1, source_target_pairs={{0,8},{8,16},{16,24},{24,32},{32,40},{40,48},{48,56},{56,64},{64,7... | collective-permute-start | bytes 11528 | tf_op jit(solution)/shard_map/ppermute | solution.py:19
  15.2 14.4 %collective-permute-start.1 = (bf16[3,256]{1,0:T(4,128)(2,1)S(1)}, bf16[3,256]{1,0:T(4,128)(2,1)S(1)}, u32[]{:S(2)}, u32[]{:S(2)}) collective-permute-start(bf16[3,256]{1,0:T(4,128)(2,1)S(1)} %slice.112), channel_id=1, source_target_pairs={{0,8},{8,16},{16,24},{24,32},{32,40},{40,48},{48,56},{56,64},{64,7... | collective-permute-start | bytes 4616 | tf_op jit(solution)/shard_map/ppermute | solution.py:19
  22.9 7.7 %copy-start.13 = (s32[512]{0:T(512)}, s32[512]{0:T(512)S(1)}, u32[]{:S(2)}) copy-start(s32[512]{0:T(512)S(1)} %broadcast_add_fusion.2) | copy-start | bytes 6148
  31.1 1.5 copy-start.8
  31.1 1.5 copy-start.9
  31.1 1.5 copy-start.10
  31.1 1.5 copy-start.11
  48.3 3.4 copy-start.1
  58.6 1.4 copy-start.7
  61.5 17.7 %copy-start.2 = (f32[256,10]{0,1:T(8,128)S(1)}, f32[256,10]{0,1:T(8,128)}, u32[]{:S(2)}) copy-start(f32[256,10]{0,1:T(8,128)} %get-tuple-element.606) | copy-start | bytes 30724 | tf_op jit(solution)/shard_map/while
  88.1 3.4 copy-start.1
  98.5 1.4 copy-start.7
  101.5 17.7 %copy-start.2 = (f32[256,10]{0,1:T(8,128)S(1)}, f32[256,10]{0,1:T(8,128)}, u32[]{:S(2)}) copy-start(f32[256,10]{0,1:T(8,128)} %get-tuple-element.606) | copy-start | bytes 30724 | tf_op jit(solution)/shard_map/while
  121.4 1.5 copy-start.6
  121.4 3.0 copy-start.19
  121.4 45.3 %copy-start.15 = (bf16[640]{0:T(1024)(128)(2,1)S(1)}, bf16[640]{0:T(1024)(128)(2,1)}, u32[]{:S(2)}) copy-start(bf16[640]{0:T(1024)(128)(2,1)} %param.36) | copy-start | bytes 3844
  121.5 273.8 %all-gather.7.cloned.1.call-start = ((), (), s32[]{:S(2)}) async-start(), calls=%async_computation.3 | async-start | bytes 17408000 | tf_op jit(solution)/shard_map/all_gather | solution.py:245
  242.5 65.3 %all-to-all-start = ((f32[8,512,320]{1,2,0:T(8,128)}), f32[8,512,320]{1,2,0:T(8,128)}, u32[]{:S(2)}, u32[]{:S(2)}) async-start(f32[8,512,320]{1,2,0:T(8,128)} %bitcast.151), calls=%async_computation | async-start | bytes 10485760 | tf_op jit(solution)/shard_map/all_to_all | solution.py:43
  329.9 5.8 %copy-start.17 = (s32[512]{0:T(512)S(1)}, s32[512]{0:T(512)}, u32[]{:S(2)}) copy-start(s32[512]{0:T(512)} %param.40) | copy-start | bytes 6148
  329.9 37.8 %all-to-all-start.1 = ((bf16[8,512,320]{1,2,0:T(8,128)(2,1)}), bf16[8,512,320]{1,2,0:T(8,128)(2,1)}, u32[]{:S(2)}, u32[]{:S(2)}) async-start(bf16[8,512,320]{1,2,0:T(8,128)(2,1)} %broadcast_in_dim.26), calls=%async_computation.1 | async-start | bytes 5242880 | tf_op jit(solution)/shard_map/all_to_all | solution.py:55
  409.8 16.7 %copy-start.14 = (s32[512]{0:T(512)S(1)}, s32[512]{0:T(512)}, u32[]{:S(2)}) copy-start(s32[512]{0:T(512)} %copy-done.13) | copy-start | bytes 6148
  409.8 36.8 %copy-start.16 = (s32[16]{0:T(128)S(1)}, s32[16]{0:T(128)}, u32[]{:S(2)}) copy-start(s32[16]{0:T(128)} %param.41) | copy-start | bytes 196
  (5 other events, 4.6 us)
Sparse Core Ops, SparseCore 0:
  121.6 83.6 all-gather.8
  207.1 188.1 all-gather.6
where the time goes:
time: 458 us; the launch traced here: 454 us
  waiting for transfers between devices  152 us (33%)
  blocking collectives  107 us (23%)
  local copies, waits for them, and re-layouts  69.2 us (15%)
  other arithmetic  44.6 us (10%)
  matrix products  40.9 us (9%)
  starting transfers between devices  20.8 us (5%)
  between operations  15.8 us (3%)
    all_to_all x1, waiting for transfers between devices, sent_and_summed(): lax.all_to_all(blocks, axis, split_axis=0, concat_axis=0, tiled=True)  59.3 us
    unnamed x1, blocking collectives  39.9 us
    all_gather x1, waiting for transfers between devices, entering(): gathered = jax.tree.map(lambda a: lax.all_gather(a, axis), part)  32.3 us
    all_to_all x1, waiting for transfers between devices, from_everyone(): lax.all_to_all(jnp.broadcast_to(array[None], (length, *array.shape)), axi...  32 us
    dynamic_update_slice x4, local copies, waits for them, and re-layouts, local(): lax.scan(advance, jnp.zeros((heads_here, HEAD_SIZE, STATE), jnp.float32),...  31.3 us
    all_gather x1, waiting for transfers between devices, local(): lax.all_gather(lm_weight, 'seq', axis=0, tiled=True)  27.6 us
    psum x1, blocking collectives, local(): square_sum = lax.psum(jnp.sum(gated * gated, axis=1), 'head')  20.6 us
    all_to_all x1, blocking collectives, from_everyone(): lax.all_to_all(jnp.broadcast_to(array[None], (length, *array.shape)), axi...  19.8 us
  transfers between devices with their start and end apart: 6, of which 4 were waited for; matrix products, arithmetic and copies ran while one was open for 10% of the time, Pallas kernels for 0%

commit v1 on v0

--- a/solution.py
+++ b/solution.py
@@ -11,6 +11,19 @@
 INNER = 5120
 EPSILON = 1e-05
 HIGH = lax.Precision.HIGHEST
+
+
+def gather_around(x, axis, dim):
+    ways = lax.axis_size(axis)
+    up = [(d, (d + 1) % ways) for d in range(ways)]
+    down = [(d, (d - 1) % ways) for d in range(ways)]
+    earlier, later = ([x], [x])
+    for _ in range(ways // 2):
+        earlier.append(lax.ppermute(earlier[-1], axis, up))
+    for _ in range((ways - 1) // 2):
+        later.append(lax.ppermute(later[-1], axis, down))
+    line = jnp.concatenate([*earlier[::-1], *later[1:]], axis=dim)
+    return jnp.roll(line, (lax.axis_index(axis) - ways // 2) * x.shape[dim], axis=dim)
 
 
 def shifted(array, axis, by):
@@ -240,11 +253,7 @@
     )
     hidden = gather_directly(hidden_part, "head", 1)
     vocab_here = lm_weight.shape[1]
-    logits = jnp.dot(
-        hidden,
-        lax.all_gather(lm_weight, "seq", axis=0, tiled=True),
-        preferred_element_type=jnp.float32,
-    )
+    logits = jnp.dot(hidden, gather_around(lm_weight, "seq", 0), preferred_element_type=jnp.float32)
     peak = jnp.max(logits, axis=1)
     total = jnp.sum(jnp.exp(logits - peak[:, None]), axis=1)
     local_target = targets - head_rank * vocab_here

time: 458 us -> 603 us (1.32)
  the two profiles are of different devices: /device:TPU:33 before, /device:TPU:40 now
where the time goes in v1:
time: 603 us; the launch traced here: 591 us
  waiting for transfers between devices  181 us (30%)
  local copies, waits for them, and re-layouts  136 us (23%)
  blocking collectives  133 us (22%)
  other arithmetic  43.3 us (7%)
  matrix products  41.3 us (7%)
  starting transfers between devices  38 us (6%)
  between operations  15.9 us (3%)
    ppermute x8, waiting for transfers between devices, gather_around(): earlier.append(lax.ppermute(earlier[-1], axis, up))  117 us
    unnamed x80, local copies, waits for them, and re-layouts  69.6 us
    unnamed x1, blocking collectives  51.9 us
    all_to_all x1, blocking collectives, from_everyone(): lax.all_to_all(jnp.broadcast_to(array[None], (length, *array.shape)), axi...  42.2 us
    all_to_all x1, waiting for transfers between devices, sent_and_summed(): lax.all_to_all(blocks, axis, split_axis=0, concat_axis=0, tiled=True)  41.4 us
    dynamic_update_slice x4, local copies, waits for them, and re-layouts, local(): lax.scan(advance, jnp.zeros((heads_here, HEAD_SIZE, STATE), jnp.float32),...  31.4 us
    all_to_all x1, waiting for transfers between devices, from_everyone(): lax.all_to_all(jnp.broadcast_to(array[None], (length, *array.shape)), axi...  22.6 us
    ppermute x7, starting transfers between devices, gather_around(): later.append(lax.ppermute(later[-1], axis, down))  21.6 us
  transfers between devices with their start and end apart: 20, of which 8 were waited for; matrix products, arithmetic and copies ran while one was open for 30% of the time, Pallas kernels for 0%

profile of v1, /device:TPU:40, one launch (start us, length us, event | category | flops | bytes accessed | tf_op | source)
XLA Modules:
  0.0 591.2 jit_solution(16166351554593533153)
XLA Ops:
  10.2 42.5 %collective-permute-done.2 = bf16[160,3200]{1,0:T(8,128)(2,1)S(1)} collective-permute-done((bf16[160,3200]{1,0:T(8,128)(2,1)}, bf16[160,3200]{1,0:T(8,128)(2,1)S(1)}, u32[]{:S(2)}, u32[]{:S(2)}) %collective-permute-start.2) | collective-permute-done | bytes 1024032 | tf_op jit(solution)/shard_map/ppermute | solution.py:22
  56.9 21.8 %collective-permute-done.3 = bf16[160,3200]{1,0:T(8,128)(2,1)S(1)} collective-permute-done((bf16[160,3200]{1,0:T(8,128)(2,1)S(1)}, bf16[160,3200]{1,0:T(8,128)(2,1)S(1)}, u32[]{:S(2)}, u32[]{:S(2)}) %collective-permute-start.3) | collective-permute-done | bytes 1024032 | tf_op jit(solution)/shard_map/ppermute | solution.py:22
  83.0 21.1 %collective-permute-done.4 = bf16[160,3200]{1,0:T(8,128)(2,1)} collective-permute-done((bf16[160,3200]{1,0:T(8,128)(2,1)S(1)}, bf16[160,3200]{1,0:T(8,128)(2,1)}, u32[]{:S(2)}, u32[]{:S(2)}) %collective-permute-start.4) | collective-permute-done | bytes 1024032 | tf_op jit(solution)/shard_map/ppermute | solution.py:22
  114.6 13.2 %collective-permute-done.5 = bf16[160,3200]{1,0:T(8,128)(2,1)} collective-permute-done((bf16[160,3200]{1,0:T(8,128)(2,1)}, bf16[160,3200]{1,0:T(8,128)(2,1)}, u32[]{:S(2)}, u32[]{:S(2)}) %collective-permute-start.5) | collective-permute-done | bytes 1024032 | tf_op jit(solution)/shard_map/ppermute | solution.py:22
  140.1 10.4 %collective-permute-done.6 = bf16[160,3200]{1,0:T(8,128)(2,1)} collective-permute-done((bf16[160,3200]{1,0:T(8,128)(2,1)}, bf16[160,3200]{1,0:T(8,128)(2,1)}, u32[]{:S(2)}, u32[]{:S(2)}) %collective-permute-start.6) | collective-permute-done | bytes 1024032 | tf_op jit(solution)/shard_map/ppermute | solution.py:22
  166.1 7.7 %collective-permute-done.7 = bf16[160,3200]{1,0:T(8,128)(2,1)} collective-permute-done((bf16[160,3200]{1,0:T(8,128)(2,1)}, bf16[160,3200]{1,0:T(8,128)(2,1)}, u32[]{:S(2)}, u32[]{:S(2)}) %collective-permute-start.7) | collective-permute-done | bytes 1024032 | tf_op jit(solution)/shard_map/ppermute | solution.py:22
  173.8 78.4 %while.46 = (s32[]{:T(128)}, f32[10,64,128]{2,1,0:T(8,128)}, f32[2,256,10,64]{1,0,3,2:T(2,128)}, f32[2,10,256]{2,0,1:T(2,128)}, f32[10]{0:T(128)}, /*index=5*/s3...) while((s32[]{:T(128)}, f32[10,64,128]{2,1,0:T(8,128)}, ...), condition=%wide.region_9.10_spmd.clone, body=%wide.region_6.9_spmd.clone.sunk | while | flops 1028866112 | bytes 7540814 | solution.py:221
  184.0 4.1 fusion.119
  195.3 14.2 %dynamic_update_slice.6 = f32[2,256,10,64]{1,0,3,2:T(2,128)} dynamic-update-slice(f32[2,256,10,64]{1,0,3,2:T(2,128)} %get-tuple-element.624, f32[1,256,10,64]{1,0,3,2:T(1,128)} %copy.129, s32[]{:T(128)} %get-tuple-element.622, s32[]{:T(128)} %constant.171.clone.1..sunk.2, s32[]{:T(128)} %constant.171.clone.1..sunk.2, s32[]{:T(128)} %constant.171.clone.1..sunk.2) | dynamic-update-slice | bytes 1310724 | tf_op jit(solution)/shard_map/while/body/jit(dynamic_update_index_in_dim)/dynamic_update_slice | solution.py:221
  223.1 4.1 fusion.119
  234.5 14.2 %dynamic_update_slice.6 = f32[2,256,10,64]{1,0,3,2:T(2,128)} dynamic-update-slice(f32[2,256,10,64]{1,0,3,2:T(2,128)} %get-tuple-element.624, f32[1,256,10,64]{1,0,3,2:T(1,128)} %copy.129, s32[]{:T(128)} %get-tuple-element.622, s32[]{:T(128)} %constant.171.clone.1..sunk.2, s32[]{:T(128)} %constant.171.clone.1..sunk.2, s32[]{:T(128)} %constant.171.clone.1..sunk.2) | dynamic-update-slice | bytes 1310724 | tf_op jit(solution)/shard_map/while/body/jit(dynamic_update_index_in_dim)/dynamic_update_slice | solution.py:221
  252.3 3.4 collective-permute-start.15
  262.0 51.9 %all-reduce = f32[160]{0:T(256)S(1)} all-reduce(f32[160]{0:T(256)S(1)} %dynamic-update-slice), channel_id=2, replica_groups=mesh['groups'=2,'seq'=16,'head'=8] {'seq'}, use_global_device_ids=true, to_apply=%add | all-reduce | flops 160 | bytes 1280
  361.7 3.7 fusion.48
  370.1 12.8 %psum.14 = f32[512]{0:T(512)S(1)} all-reduce(f32[512]{0:T(512)S(1)} %multiply_reduce_fusion), channel_id=1, replica_groups=mesh['groups'=2,'seq'=16,'head'=8] {'head'}, use_global_device_ids=true, to_apply=%region_16.17 | all-reduce | flops 512 | bytes 4096 | tf_op jit(solution)/shard_map/psum | solution.py:240
  383.0 6.4 %fusion.63 = f32[512,2560]{0,1:T(8,128)} fusion(bf16[640,2560]{1,0:T(8,128)(2,1)S(1)} %copy-done, f32[640]{0:T(1024)S(1)} %copy-done.19, f32[512]{0:T(512)S(1)} %add_rsqrt_fusion.1, f32[512,640]{1,0:T(8,128)} %copy.90, bf16[512,640]{1,0:T(8,128)(2,1)} %param.27), kind=kOutput, calls=%fused_computation.99 | convolution fusion | flops 1680670720 | bytes 10490368 | tf_op jit(solution)/shard_map/dot_general | solution.py:243
  389.4 4.8 all-to-all-start
  413.6 41.4 %all-to-all-done = f32[8,512,320]{1,2,0:T(8,128)} async-done(((f32[8,512,320]{1,2,0:T(8,128)}), f32[8,512,320]{1,2,0:T(8,128)}, u32[]{:S(2)}, u32[]{:S(2)}) %all-to-all-start) | async-done | bytes 5242912 | tf_op jit(solution)/shard_map/all_to_all | solution.py:56
  458.3 12.7 %psum.15 = f32[512]{0:T(512)S(1)} all-reduce(f32[512]{0:T(512)S(1)} %get-tuple-element.424), channel_id=1, replica_groups=mesh['groups'=2,'seq'=16,'head'=8] {'head'}, use_global_device_ids=true, to_apply=%region_19.20 | all-reduce | flops 512 | bytes 4096 | tf_op jit(solution)/shard_map/psum | solution.py:248
  472.9 4.9 all-to-all-start.1
  488.0 22.6 %all-to-all-done.1 = bf16[8,512,320]{1,2,0:T(8,128)(2,1)} async-done(((bf16[8,512,320]{1,2,0:T(8,128)(2,1)}), bf16[8,512,320]{1,2,0:T(8,128)(2,1)}, u32[]{:S(2)}, u32[]{:S(2)}) %all-to-all-start.1) | async-done | bytes 2621472 | tf_op jit(solution)/shard_map/all_to_all | solution.py:68
  510.6 14.8 %fusion.92 = (f32[512]{0:T(512)S(1)}, f32[512,3200]{1,0:T(8,128)S(1)}) fusion(bf16[512,2560]{0,1:T(8,128)(2,1)} %bitcast.23, bf16[5120,3200]{1,0:T(8,128)(2,1)} %constant_dynamic-update-slice_fusion, s32[]{:T(128)S(6)} %select_n.57), kind=kOutput, calls=%fused_computation.205 | convolution fusion | flops 8390245888 | bytes 25561092 | tf_op jit(solution)/shard_map/dot_general | solution.py:256
  527.4 12.9 %all-gather.3 = f32[8,3,512]{2,1,0:T(4,128)S(1)} all-gather(f32[1,3,512]{2,1,0:T(4,128)S(1)} %maximum_bitcast_fusion), channel_id=4, replica_groups=mesh['groups'=2,'seq'=16,'head'=8] {'head'}, dimensions={0}, use_global_device_ids=true | all-gather | bytes 55296 | tf_op jit(solution)/shard_map/all_gather | solution.py:85
  541.4 42.2 %all_to_all.16 = f32[16,1,16]{2,1,0:T(1,128)S(1)} all-to-all(f32[16,1,16]{2,1,0:T(1,128)S(1)} %broadcast_in_dim.28), channel_id=1, replica_groups=mesh['groups'=2,'seq'=16,'head'=8] {'seq'}, dimensions={0} | all-to-all | bytes 2048 | tf_op jit(solution)/shard_map/all_to_all | solution.py:68
  (258 shorter events, 185.3 us)
Async XLA Ops:
  7.2 375.8 %copy-start = (bf16[640,2560]{1,0:T(8,128)(2,1)S(1)}, bf16[640,2560]{1,0:T(8,128)(2,1)}, u32[]{:S(2)}) copy-start(bf16[640,2560]{1,0:T(8,128)(2,1)} %param.37) | copy-start | bytes 9830404
  7.2 353.7 %all-gather.6.cloned.1.call-start = ((), (), s32[]{:S(2)}) async-start(), calls=%async_computation.3 | async-start | bytes 5570560 | tf_op jit(solution)/shard_map/all_gather | solution.py:37
  7.3 45.4 %collective-permute-start.2 = (bf16[160,3200]{1,0:T(8,128)(2,1)}, bf16[160,3200]{1,0:T(8,128)(2,1)S(1)}, u32[]{:S(2)}, u32[]{:S(2)}) collective-permute-start(bf16[160,3200]{1,0:T(8,128)(2,1)} %param.39), channel_id=1, source_target_pairs={{0,8},{8,16},{16,24},{24,32},{32,40},{40,48},{48,56},{56,64},{64,7... | collective-permute-start | bytes 3072008 | tf_op jit(solution)/shard_map/ppermute | solution.py:22
  53.7 25.1 %collective-permute-start.3 = (bf16[160,3200]{1,0:T(8,128)(2,1)S(1)}, bf16[160,3200]{1,0:T(8,128)(2,1)S(1)}, u32[]{:S(2)}, u32[]{:S(2)}) collective-permute-start(bf16[160,3200]{1,0:T(8,128)(2,1)S(1)} %collective-permute-done.2), channel_id=1, source_target_pairs={{0,8},{8,16},{16,24},{24,32},{32,40},{40,48},{48,56},{56,64},{64,7... | collective-permute-start | bytes 3072008 | tf_op jit(solution)/shard_map/ppermute | solution.py:22
  53.7 26.1 %collective-permute-start.10 = (bf16[160,3200]{1,0:T(8,128)(2,1)}, bf16[160,3200]{1,0:T(8,128)(2,1)}, u32[]{:S(2)}, u32[]{:S(2)}) collective-permute-start(bf16[160,3200]{1,0:T(8,128)(2,1)} %param.39), channel_id=1, source_target_pairs={{0,120},{8,0},{16,8},{24,16},{32,24},{40,32},{48,40},{56,48},{64,5... | collective-permute-start | bytes 3072008 | tf_op jit(solution)/shard_map/ppermute | solution.py:24
  79.7 24.3 %collective-permute-start.4 = (bf16[160,3200]{1,0:T(8,128)(2,1)S(1)}, bf16[160,3200]{1,0:T(8,128)(2,1)}, u32[]{:S(2)}, u32[]{:S(2)}) collective-permute-start(bf16[160,3200]{1,0:T(8,128)(2,1)S(1)} %collective-permute-done.3), channel_id=1, source_target_pairs={{0,8},{8,16},{16,24},{24,32},{32,40},{40,48},{48,56},{56,64},{64,7... | collective-permute-start | bytes 3072008 | tf_op jit(solution)/shard_map/ppermute | solution.py:22
  79.7 32.0 %collective-permute-start.11 = (bf16[160,3200]{1,0:T(8,128)(2,1)}, bf16[160,3200]{1,0:T(8,128)(2,1)}, u32[]{:S(2)}, u32[]{:S(2)}) collective-permute-start(bf16[160,3200]{1,0:T(8,128)(2,1)} %collective-permute-done.10), channel_id=1, source_target_pairs={{0,120},{8,0},{16,8},{24,16},{32,24},{40,32},{48,40},{56,48},{64,5... | collective-permute-start | bytes 3072008 | tf_op jit(solution)/shard_map/ppermute | solution.py:24
  104.1 23.7 %collective-permute-start.5 = (bf16[160,3200]{1,0:T(8,128)(2,1)}, bf16[160,3200]{1,0:T(8,128)(2,1)}, u32[]{:S(2)}, u32[]{:S(2)}) collective-permute-start(bf16[160,3200]{1,0:T(8,128)(2,1)} %collective-permute-done.4), channel_id=1, source_target_pairs={{0,8},{8,16},{16,24},{24,32},{32,40},{40,48},{48,56},{56,64},{64,7... | collective-permute-start | bytes 3072008 | tf_op jit(solution)/shard_map/ppermute | solution.py:22
  105.4 46.8 %collective-permute-start = (bf16[3,640]{1,0:T(4,128)(2,1)}, bf16[3,640]{1,0:T(4,128)(2,1)}, u32[]{:S(2)}, u32[]{:S(2)}) collective-permute-start(bf16[3,640]{1,0:T(4,128)(2,1)} %slice.103), channel_id=1, source_target_pairs={{0,8},{8,16},{16,24},{24,32},{32,40},{40,48},{48,56},{56,64},{64,7... | collective-permute-start | bytes 11528 | tf_op jit(solution)/shard_map/ppermute | solution.py:32
  107.9 27.8 %collective-permute-start.1 = (bf16[3,256]{1,0:T(4,128)(2,1)S(1)}, bf16[3,256]{1,0:T(4,128)(2,1)S(1)}, u32[]{:S(2)}, u32[]{:S(2)}) collective-permute-start(bf16[3,256]{1,0:T(4,128)(2,1)S(1)} %slice.112), channel_id=1, source_target_pairs={{0,8},{8,16},{16,24},{24,32},{32,40},{40,48},{48,56},{56,64},{64,7... | collective-permute-start | bytes 4616 | tf_op jit(solution)/shard_map/ppermute | solution.py:32
  111.8 25.0 %collective-permute-start.12 = (bf16[160,3200]{1,0:T(8,128)(2,1)}, bf16[160,3200]{1,0:T(8,128)(2,1)}, u32[]{:S(2)}, u32[]{:S(2)}) collective-permute-start(bf16[160,3200]{1,0:T(8,128)(2,1)} %collective-permute-done.11), channel_id=1, source_target_pairs={{0,120},{8,0},{16,8},{24,16},{32,24},{40,32},{48,40},{56,48},{64,5... | collective-permute-start | bytes 3072008 | tf_op jit(solution)/shard_map/ppermute | solution.py:24
  127.7 22.8 %collective-permute-start.6 = (bf16[160,3200]{1,0:T(8,128)(2,1)}, bf16[160,3200]{1,0:T(8,128)(2,1)}, u32[]{:S(2)}, u32[]{:S(2)}) collective-permute-start(bf16[160,3200]{1,0:T(8,128)(2,1)} %collective-permute-done.5), channel_id=1, source_target_pairs={{0,8},{8,16},{16,24},{24,32},{32,40},{40,48},{48,56},{56,64},{64,7... | collective-permute-start | bytes 3072008 | tf_op jit(solution)/shard_map/ppermute | solution.py:22
  136.8 26.1 %collective-permute-start.13 = (bf16[160,3200]{1,0:T(8,128)(2,1)}, bf16[160,3200]{1,0:T(8,128)(2,1)}, u32[]{:S(2)}, u32[]{:S(2)}) collective-permute-start(bf16[160,3200]{1,0:T(8,128)(2,1)} %collective-permute-done.12), channel_id=1, source_target_pairs={{0,120},{8,0},{16,8},{24,16},{32,24},{40,32},{48,40},{56,48},{64,5... | collective-permute-start | bytes 3072008 | tf_op jit(solution)/shard_map/ppermute | solution.py:24
  150.6 23.3 %collective-permute-start.7 = (bf16[160,3200]{1,0:T(8,128)(2,1)}, bf16[160,3200]{1,0:T(8,128)(2,1)}, u32[]{:S(2)}, u32[]{:S(2)}) collective-permute-start(bf16[160,3200]{1,0:T(8,128)(2,1)} %collective-permute-done.6), channel_id=1, source_target_pairs={{0,8},{8,16},{16,24},{24,32},{32,40},{40,48},{48,56},{56,64},{64,7... | collective-permute-start | bytes 3072008 | tf_op jit(solution)/shard_map/ppermute | solution.py:22
  162.9 89.4 %collective-permute-start.14 = (bf16[160,3200]{1,0:T(8,128)(2,1)}, bf16[160,3200]{1,0:T(8,128)(2,1)}, u32[]{:S(2)}, u32[]{:S(2)}) collective-permute-start(bf16[160,3200]{1,0:T(8,128)(2,1)} %collective-permute-done.13), channel_id=1, source_target_pairs={{0,120},{8,0},{16,8},{24,16},{32,24},{40,32},{48,40},{56,48},{64,5... | collective-permute-start | bytes 3072008 | tf_op jit(solution)/shard_map/ppermute | solution.py:24
  173.8 81.8 %collective-permute-start.8 = (bf16[160,3200]{1,0:T(8,128)(2,1)}, bf16[160,3200]{1,0:T(8,128)(2,1)}, u32[]{:S(2)}, u32[]{:S(2)}) collective-permute-start(bf16[160,3200]{1,0:T(8,128)(2,1)} %collective-permute-done.7), channel_id=1, source_target_pairs={{0,8},{8,16},{16,24},{24,32},{32,40},{40,48},{48,56},{56,64},{64,7... | collective-permute-start | bytes 3072008 | tf_op jit(solution)/shard_map/ppermute | solution.py:22
  252.3 71.3 %collective-permute-start.15 = (bf16[160,3200]{1,0:T(8,128)(2,1)}, bf16[160,3200]{1,0:T(8,128)(2,1)}, u32[]{:S(2)}, u32[]{:S(2)}) collective-permute-start(bf16[160,3200]{1,0:T(8,128)(2,1)} %collective-permute-done.14), channel_id=1, source_target_pairs={{0,120},{8,0},{16,8},{24,16},{32,24},{40,32},{48,40},{56,48},{64,5... | collective-permute-start | bytes 3072008 | tf_op jit(solution)/shard_map/ppermute | solution.py:24
  255.6 70.4 %collective-permute-start.9 = (bf16[160,3200]{1,0:T(8,128)(2,1)}, bf16[160,3200]{1,0:T(8,128)(2,1)}, u32[]{:S(2)}, u32[]{:S(2)}) collective-permute-start(bf16[160,3200]{1,0:T(8,128)(2,1)} %collective-permute-done.8), channel_id=1, source_target_pairs={{0,8},{8,16},{16,24},{24,32},{32,40},{40,48},{48,56},{56,64},{64,7... | collective-permute-start | bytes 3072008 | tf_op jit(solution)/shard_map/ppermute | solution.py:22
  323.5 33.1 %collective-permute-start.16 = (bf16[160,3200]{1,0:T(8,128)(2,1)}, bf16[160,3200]{1,0:T(8,128)(2,1)S(1)}, u32[]{:S(2)}, u32[]{:S(2)}) collective-permute-start(bf16[160,3200]{1,0:T(8,128)(2,1)} %collective-permute-done.15), channel_id=1, source_target_pairs={{0,120},{8,0},{16,8},{24,16},{32,24},{40,32},{48,40},{56,48},{64,5... | collective-permute-start | bytes 3072008 | tf_op jit(solution)/shard_map/ppermute | solution.py:24
  389.4 65.6 %all-to-all-start = ((f32[8,512,320]{1,2,0:T(8,128)}), f32[8,512,320]{1,2,0:T(8,128)}, u32[]{:S(2)}, u32[]{:S(2)}) async-start(f32[8,512,320]{1,2,0:T(8,128)} %bitcast.150), calls=%async_computation | async-start | bytes 10485760 | tf_op jit(solution)/shard_map/all_to_all | solution.py:56
  406.8 51.3 %copy-start.16 = (bf16[512,320]{0,1:T(8,128)(2,1)S(1)}, bf16[512,320]{0,1:T(8,128)(2,1)}, u32[]{:S(2)}) copy-start(bf16[512,320]{0,1:T(8,128)(2,1)} %param.24) | copy-start | bytes 983044
  472.9 37.6 %all-to-all-start.1 = ((bf16[8,512,320]{1,2,0:T(8,128)(2,1)}), bf16[8,512,320]{1,2,0:T(8,128)(2,1)}, u32[]{:S(2)}, u32[]{:S(2)}) async-start(bf16[8,512,320]{1,2,0:T(8,128)(2,1)} %broadcast_in_dim.26), calls=%async_computation.1 | async-start | bytes 5242880 | tf_op jit(solution)/shard_map/all_to_all | solution.py:68
  510.6 73.6 %copy-start.1 = (bf16[640,2560]{1,0:T(8,128)(2,1)S(1)}, bf16[640,2560]{1,0:T(8,128)(2,1)}, u32[]{:S(2)}) copy-start(bf16[640,2560]{1,0:T(8,128)(2,1)} %param.37) | copy-start | bytes 9830404
  525.4 58.2 %copy-start.20 = (s32[16]{0:T(128)S(1)}, s32[16]{0:T(128)}, u32[]{:S(2)}) copy-start(s32[16]{0:T(128)} %param.41) | copy-start | bytes 196
  (18 other events, 198.4 us)
Sparse Core Ops, SparseCore 0:
  252.4 92.0 all-gather.5
